TPU v7x, 32 devices: a whole 2x2x4 slice. The times are simulated.
32 devices in a mesh: dp: 8 (over z, x), tensor: 4 (over y, core).
Axes of the slice: x: 2, y: 2, z: 4, core: 2. Of those that a mesh axis runs over, the one named last changes fastest.
Arguments:
- tokens: bfloat16 [16, 128, 2048], P('dp'), may hold values from -6 to 6
- cotangent: bfloat16 [16, 128, 2048], P('dp'), may hold values from -6 to 6
- routes: int32 [16, 128, 4], P('dp'), may hold values from 0 to 5, as said below
- gates: bfloat16 [16, 128, 4], P('dp'), may hold values from 0.099609375 to 0.5
- lengths: int32 [16], P('dp'), may hold values from 64 to 128, as said below
- deal: int32 [16], replicated, may hold values from 0 to 15, as said below
- norm1_gain: float32 [2048], P('dp'), may hold values from 0.1 to 1.9
- q_weight: float32 [2048, 2048], P('dp', 'tensor'), may hold values from -0.125 to 0.125
- q_bias: float32 [16, 128], P('tensor', 'dp'), may hold values from -3 to 3
- k_weight: float32 [2048, 2048], P('dp', 'tensor'), may hold values from -0.125 to 0.125
- v_weight: float32 [2048, 2048], P('dp', 'tensor'), may hold values from -0.125 to 0.125
- v_bias: float32 [16, 128], P('tensor', 'dp'), may hold values from -3 to 3
- o_weight: float32 [2048, 2048], P('tensor', 'dp'), may hold values from -0.75 to 0.75
- norm2_gain: float32 [2048], P('dp'), may hold values from 0.1 to 1.9
- expert_gate: float32 [6, 2048, 1408], P(None, 'dp', 'tensor'), may hold values from -0.125 to 0.125
- expert_up: float32 [6, 2048, 1408], P(None, 'dp', 'tensor'), may hold values from -0.125 to 0.125
- expert_down: float32 [6, 1408, 2048], P(None, 'tensor', 'dp'), may hold values from -0.21875 to 0.21875
- shared_gate: float32 [2048, 5632], P('dp', 'tensor'), may hold values from -0.125 to 0.125
- shared_up: float32 [2048, 5632], P('dp', 'tensor'), may hold values from -0.125 to 0.125
- shared_down: float32 [5632, 2048], P('tensor', 'dp'), may hold values from -0.109375 to 0.109375
- shared_switch: float32 [2048], P('dp'), may hold values from -0.125 to 0.125
Outputs:
- output: float32 [16, 128, 2048], P('dp', None, 'tensor')
- tokens_grad: float32 [16, 128, 2048], P('dp', None, 'tensor')
- norm1_gain_grad: float32 [2048], P('dp')
- q_weight_grad: float32 [2048, 2048], P('dp', 'tensor')
- q_bias_grad: float32 [16, 128], P('tensor', 'dp')
- k_weight_grad: float32 [2048, 2048], P('dp', 'tensor')
- v_weight_grad: float32 [2048, 2048], P('dp', 'tensor')
- v_bias_grad: float32 [16, 128], P('tensor', 'dp')
- o_weight_grad: float32 [2048, 2048], P('tensor', 'dp')
- norm2_gain_grad: float32 [2048], P('dp')
- expert_gate_grad: float32 [6, 2048, 1408], P(None, 'dp', 'tensor')
- expert_up_grad: float32 [6, 2048, 1408], P(None, 'dp', 'tensor')
- expert_down_grad: float32 [6, 1408, 2048], P(None, 'tensor', 'dp')
- shared_gate_grad: float32 [2048, 5632], P('dp', 'tensor')
- shared_up_grad: float32 [2048, 5632], P('dp', 'tensor')
- shared_down_grad: float32 [5632, 2048], P('tensor', 'dp')
- shared_switch_grad: float32 [2048], P('dp')
Inputs may be any that keep to these rules, and one draw needn't show every extreme that they name: Sequences 2i and 2i+1 are given on dp index i. The two sequences dealt to one dp index have lengths adding up to exactly 192. `deal`: dealt slot 2i holds sequence 2i; the odd sequences move by one common rotation of the dp indices: slot 2i+1 holds sequence 2((i - r) mod the number of dp indices) + 1, for one r of the draw. `routes`: each row names 4 different experts. Among the 192 real tokens dealt to one dp index, every expert is named by exactly 128 tokens. Rows past a sequence's length hold valid ids too.
All inputs are finite; a program needn't handle non-finite values.
Results may differ from a plain program's by a relative error of at most 0.013.
The roundings to bfloat16 on the way count: a program that leaves them out, or rounds other values in their place, can miss the bound.
Values may be sent and summed in bfloat16 or wider, within the bound.
A program may use at most 256 MiB of HBM per device.

v0:
```python
from functools import partial
import jax
import jax.numpy as jnp
from jax import lax
from jax.sharding import PartitionSpec as P

HEAD_DIM = 128
EPSILON = 1e-06
NEGATIVE = -1e30
LANES = 128
BF16 = jnp.bfloat16
F32 = jnp.float32
ALL = ("dp", "tensor")


def normalize(values, gain):
    return values * lax.rsqrt(jnp.mean(values * values, axis=-1, keepdims=True) + EPSILON) * gain


def nt(left, right):
    return lax.dot_general(left, right, (((1,), (1,)), ((), ())), preferred_element_type=F32)


def tn(left, right):
    return lax.dot_general(left, right, (((0,), (0,)), ((), ())), preferred_element_type=F32)


def nn(left, right):
    return lax.dot_general(left, right, (((1,), (0,)), ((), ())), preferred_element_type=F32)


def gather_all(value):
    return lax.all_gather(value, ALL, axis=0, tiled=True)


def scatter_all(value):
    return lax.psum_scatter(value, ALL, scatter_dimension=0, tiled=True)


def exchange_dp(value):
    return lax.all_to_all(value, "dp", 0, 0, tiled=False)


def per_device(
    tokens,
    cotangent,
    routes,
    gates,
    lengths,
    deal,
    norm1_gain,
    q_weight,
    q_bias,
    k_weight,
    v_weight,
    v_bias,
    o_weight,
    norm2_gain,
    expert_gate,
    expert_up,
    expert_down,
    shared_gate,
    shared_up,
    shared_down,
    shared_switch,
):
    n_dp = lax.axis_size("dp")
    n_tensor = lax.axis_size("tensor")
    place = lax.axis_index("dp")
    member = lax.axis_index("tensor")
    seqs, span, width = tokens.shape
    rows = seqs * span
    shard = rows // n_tensor
    experts, slice_d, expert_cols = expert_gate.shape
    shared_cols = shared_gate.shape[1]
    head_cols = q_weight.shape[1]
    heads = head_cols // HEAD_DIM

    def own_rows(value):
        return lax.dynamic_slice_in_dim(value, member * shard, shard, 0)

    valid = (jnp.arange(span)[None, :] < lengths[:, None]).reshape(rows, 1)
    dense = jnp.zeros((seqs, span, LANES), F32)
    for rank in range(routes.shape[-1]):
        hit = routes[..., rank, None] == jnp.arange(LANES)
        dense = dense + jnp.where(hit, gates[..., rank, None].astype(F32), 0.0)
    dense = dense.reshape(rows, LANES).astype(BF16)
    cot = jnp.where(valid, cotangent.reshape(rows, width), 0).astype(BF16)
    cot_packed = gather_all(own_rows(jnp.concatenate([cot, dense], axis=1)))
    small = jnp.concatenate(
        [norm1_gain, norm2_gain, shared_switch, q_bias.reshape(-1), v_bias.reshape(-1)]
    ).astype(BF16)
    small = lax.all_gather(small[None, :], "dp", axis=0, tiled=True)
    gain_one = small[:, :slice_d].reshape(-1).astype(F32)
    gain_two = small[:, slice_d : 2 * slice_d].reshape(-1).astype(F32)
    switch = small[:, 2 * slice_d : 3 * slice_d].reshape(1, -1)
    piece = q_bias.shape[1]

    def whole_bias(start):
        part = small[:, start : start + heads * piece].reshape(n_dp, heads, piece)
        return part.transpose(1, 0, 2).reshape(-1).astype(F32)

    bias_q = whole_bias(3 * slice_d)
    bias_v = whole_bias(3 * slice_d + heads * piece)
    attn_weights = jnp.concatenate(
        [
            q_weight.astype(BF16),
            k_weight.astype(BF16),
            v_weight.astype(BF16),
            o_weight.T.astype(BF16),
        ],
        axis=1,
    )
    attn_weights = lax.all_gather(attn_weights, "dp", axis=0, tiled=True)
    weight_qkv = attn_weights[:, : 3 * head_cols]
    weight_o = attn_weights[:, 3 * head_cols :]

    def by_unit(expert_part, shared_part):
        return jnp.concatenate(
            [
                expert_part.astype(BF16).reshape(n_dp, -1, slice_d),
                shared_part.astype(BF16).reshape(n_dp, -1, slice_d),
            ],
            axis=1,
        )

    gate_sent = by_unit(
        expert_gate.astype(BF16).transpose(0, 2, 1).reshape(-1, slice_d), shared_gate.astype(BF16).T
    )
    up_sent = by_unit(
        expert_up.astype(BF16).transpose(0, 2, 1).reshape(-1, slice_d), shared_up.astype(BF16).T
    )
    down_sent = by_unit(expert_down.reshape(-1, slice_d), shared_down)
    arrived = exchange_dp(jnp.stack([gate_sent, up_sent, down_sent], axis=1))
    units = arrived.shape[2]
    routed = experts * expert_cols // n_dp
    arrived = arrived.transpose(1, 2, 0, 3).reshape(3, units, width)
    gate_units, up_units, down_units = (arrived[0], arrived[1], arrived[2])
    inputs = tokens.reshape(rows, width).astype(F32)
    inputs_own = own_rows(inputs)
    normed_one = normalize(inputs, gain_one).astype(BF16)
    projected = nn(normed_one, weight_qkv)
    head_shape = (seqs, span, heads, HEAD_DIM)
    queries = (projected[:, :head_cols] + bias_q).astype(BF16).reshape(head_shape)
    keys = projected[:, head_cols : 2 * head_cols].astype(BF16).reshape(head_shape)
    values = (projected[:, 2 * head_cols :] + bias_v).astype(BF16).reshape(head_shape)
    order = jnp.arange(span)
    causal = order[None, :] <= order[:, None]
    scale = HEAD_DIM ** (-0.5)
    scores = jnp.einsum("bqhd,bkhd->bhqk", queries, keys, preferred_element_type=F32) * scale
    scores = jnp.where(causal, scores, NEGATIVE)
    top = jnp.max(scores, axis=-1, keepdims=True)
    powers = jnp.exp(scores - top)
    probs = powers / jnp.sum(powers, axis=-1, keepdims=True)
    probs_low = probs.astype(BF16)
    attended = (
        jnp.einsum("bhqk,bkhd->bqhd", probs_low, values, preferred_element_type=F32)
        .reshape(rows, -1)
        .astype(BF16)
    )
    attn_part = nt(attended, weight_o)
    middle = inputs_own + lax.psum_scatter(attn_part, "tensor", scatter_dimension=0, tiled=True)
    normed_two = gather_all(normalize(middle, gain_two).astype(BF16))
    cot_all = cot_packed[:, :width]
    route_share = cot_packed[:, width : width + LANES]
    unit_expert = (place * routed + jnp.arange(routed)) // expert_cols
    picks = (jnp.arange(LANES)[:, None] == unit_expert[None, :]).astype(BF16)
    gate_logit = nt(normed_two, switch)
    switch_gate = jax.nn.sigmoid(gate_logit)
    share = jnp.concatenate(
        [
            nn(route_share, picks),
            jnp.broadcast_to(switch_gate, (switch_gate.shape[0], units - routed)),
        ],
        axis=1,
    )
    gate_act = nt(normed_two, gate_units)
    up_act = nt(normed_two, up_units)
    logistic = jax.nn.sigmoid(gate_act)
    silu = gate_act * logistic
    inner = (silu * up_act).astype(BF16).astype(F32)
    inner_share = (inner * share).astype(BF16)
    mixed = nn(inner_share, down_units).astype(BF16)
    mixed = lax.psum_scatter(mixed, "dp", scatter_dimension=0, tiled=True)
    mixed = lax.psum_scatter(mixed, "tensor", scatter_dimension=1, tiled=True)
    grad_inner_raw = nt(cot_all, down_units)
    grad_logit = (
        jnp.sum(inner[:, routed:] * grad_inner_raw[:, routed:], axis=1, keepdims=True)
        * switch_gate
        * (1.0 - switch_gate)
    )
    grad_inner = grad_inner_raw * share
    slope = logistic * (1.0 + gate_act * (1.0 - logistic))
    grad_gate_act = (grad_inner * up_act * slope).astype(BF16)
    grad_up_act = (grad_inner * silu).astype(BF16)
    back_two = nn(grad_gate_act, gate_units) + nn(grad_up_act, up_units)
    back_two = (back_two + grad_logit * switch.astype(F32)).astype(BF16)
    back_two = scatter_all(back_two).astype(F32)
    grad_down = tn(inner_share, cot_all)
    grad_gate = tn(grad_gate_act, normed_two)
    grad_up = tn(grad_up_act, normed_two)
    grad_switch = jnp.sum(grad_logit * normed_two.astype(F32), axis=0)
    sent_back = jnp.stack([grad_gate, grad_up, grad_down]).astype(BF16)
    sent_back = sent_back.reshape(3, units, n_dp, slice_d).transpose(2, 0, 1, 3)
    returned = exchange_dp(sent_back).astype(F32)

    def split_units(value):
        routed_part = value[:, :routed].reshape(experts, expert_cols, slice_d)
        return (routed_part, value[:, routed:].reshape(shared_cols, slice_d))

    grad_gate_experts, grad_gate_shared = split_units(returned[:, 0])
    grad_up_experts, grad_up_shared = split_units(returned[:, 1])
    grad_down_experts, grad_down_shared = split_units(returned[:, 2])
    unused_two, norm_two_back = jax.vjp(normalize, middle, gain_two)
    grad_middle_norm, grad_gain_two = norm_two_back(back_two)
    grad_middle = own_rows(cot).astype(F32) + grad_middle_norm
    grad_attn = lax.all_gather(grad_middle.astype(BF16), "tensor", axis=0, tiled=True)
    grad_weight_o = tn(grad_attn, attended)
    grad_attended = nn(grad_attn, weight_o).astype(BF16).reshape(head_shape)
    grad_values = (
        jnp.einsum("bhqk,bqhd->bkhd", probs_low, grad_attended, preferred_element_type=F32)
        .astype(BF16)
        .reshape(rows, -1)
    )
    grad_probs = jnp.einsum("bqhd,bkhd->bhqk", grad_attended, values, preferred_element_type=F32)
    grad_scores = (
        probs * (grad_probs - jnp.sum(grad_probs * probs, axis=-1, keepdims=True))
    ).astype(BF16)
    grad_queries = (
        (jnp.einsum("bhqk,bkhd->bqhd", grad_scores, keys, preferred_element_type=F32) * scale)
        .astype(BF16)
        .reshape(rows, -1)
    )
    grad_keys = (
        (jnp.einsum("bhqk,bqhd->bkhd", grad_scores, queries, preferred_element_type=F32) * scale)
        .astype(BF16)
        .reshape(rows, -1)
    )
    grad_qkv = jnp.concatenate([grad_queries, grad_keys, grad_values], axis=1)
    grad_attn_weights = jnp.concatenate([tn(normed_one, grad_qkv), grad_weight_o], axis=1).astype(
        BF16
    )
    grad_attn_weights = lax.psum_scatter(
        grad_attn_weights, "dp", scatter_dimension=0, tiled=True
    ).astype(F32)
    back_one = nt(grad_qkv, weight_qkv)
    back_one = lax.psum_scatter(back_one, "tensor", scatter_dimension=0, tiled=True)
    unused_one, norm_one_back = jax.vjp(normalize, inputs_own, gain_one)
    grad_input_norm, grad_gain_one = norm_one_back(back_one)
    grad_input = grad_middle + grad_input_norm
    bias_part = jnp.concatenate(
        [
            jnp.sum(grad_queries.astype(F32), axis=0).reshape(heads, n_dp, piece),
            jnp.sum(grad_values.astype(F32), axis=0).reshape(heads, n_dp, piece),
        ],
        axis=0,
    )
    bias_part = bias_part.transpose(1, 0, 2).reshape(1, n_dp, -1)
    mine = (jnp.arange(n_tensor) == member)[:, None, None]
    bias_part = jnp.where(mine, bias_part, 0.0)
    gains = jnp.concatenate([grad_gain_one, grad_gain_two, grad_switch])
    gains = gains.reshape(1, 3, n_dp, slice_d).transpose(0, 2, 1, 3).reshape(n_dp, 3 * slice_d)
    pack = jnp.concatenate([gains, bias_part.transpose(1, 0, 2).reshape(n_dp, -1)], axis=1)
    pack = lax.psum(pack, ALL)
    pack = lax.dynamic_slice_in_dim(pack, place, 1, 0)[0]
    bias_own = lax.dynamic_slice_in_dim(
        pack[3 * slice_d :].reshape(n_tensor, 2, heads, piece), member, 1, 0
    )[0]

    def to_columns(value):
        return lax.all_to_all(value, "tensor", 1, 0, tiled=True)

    out_shape = (seqs, span, width // n_tensor)
    output = jnp.where(valid, to_columns(middle) + mixed.astype(F32), 0.0).reshape(out_shape)
    tokens_grad = jnp.where(valid, to_columns(grad_input), 0.0).reshape(out_shape)
    return (
        output,
        tokens_grad,
        pack[:slice_d],
        grad_attn_weights[:, :head_cols],
        bias_own[0],
        grad_attn_weights[:, head_cols : 2 * head_cols],
        grad_attn_weights[:, 2 * head_cols : 3 * head_cols],
        bias_own[1],
        grad_attn_weights[:, 3 * head_cols :].T,
        pack[slice_d : 2 * slice_d],
        grad_gate_experts.transpose(0, 2, 1),
        grad_up_experts.transpose(0, 2, 1),
        grad_down_experts,
        grad_gate_shared.T,
        grad_up_shared.T,
        grad_down_shared,
        pack[2 * slice_d : 3 * slice_d],
    )


IN_SPECS = (
    P("dp", None, None),
    P("dp", None, None),
    P("dp", None, None),
    P("dp", None, None),
    P("dp"),
    P(),
    P("dp"),
    P("dp", "tensor"),
    P("tensor", "dp"),
    P("dp", "tensor"),
    P("dp", "tensor"),
    P("tensor", "dp"),
    P("tensor", "dp"),
    P("dp"),
    P(None, "dp", "tensor"),
    P(None, "dp", "tensor"),
    P(None, "tensor", "dp"),
    P("dp", "tensor"),
    P("dp", "tensor"),
    P("tensor", "dp"),
    P("dp"),
)
OUT_SPECS = (P("dp", None, "tensor"), P("dp", None, "tensor")) + IN_SPECS[6:]


def solution(mesh):
    return jax.shard_map(
        per_device, mesh=mesh, in_specs=IN_SPECS, out_specs=OUT_SPECS, check_vma=False
    )
```

profile of v0, /device:TPU:0, one launch (start us, length us, event | category | flops | bytes accessed | tf_op | source)
XLA Modules:
  0.0 1104.9 jit_solution(10503144483082694511)
XLA Ops:
  13.3 33.5 %all-gather = bf16[8,1,896]{2,1,0:T(2,128)(2,1)S(1)} all-gather(bf16[1,1,896]{2,1,0:T(2,128)(2,1)S(1)} %bitcast.258), channel_id=1, replica_groups=mesh['dp'=8,'tensor'=4] {'dp'}, dimensions={0}, use_global_device_ids=true | all-gather | bytes 16128 | tf_op jit(solution)/shard_map/all_gather | solution.py:93
  49.2 91.7 %all-gather.6.cloned.1.call-done = bf16[2048,2048]{0,1:T(8,128)(2,1)} async-done(((bf16[256,2048]{0,1:T(8,128)(2,1)}), bf16[2048,2048]{0,1:T(8,128)(2,1)}) %all-gather.6.cloned.1.call-update) | async-done | bytes 8388624 | tf_op jit(solution)/shard_map/all_gather | solution.py:114
  140.9 4.6 fusion.7
  149.5 3.6 fusion.18
  156.4 26.3 %reduce-scatter.7.cloned.1.call-done = f32[64,2048]{1,0:T(8,128)} async-done(((f32[256,2048]{1,0:T(8,128)}), f32[64,2048]{1,0:T(8,128)}) %reduce-scatter.7.cloned.1.call-update) | async-done | bytes 524304 | tf_op jit(solution)/shard_map/reduce_scatter | solution.py:162
  200.5 5.5 all-to-all-start.1
  206.3 145.4 %all-to-all-done.1 = bf16[8,3,440,256]{3,2,1,0:T(8,128)(2,1)} async-done(((bf16[8,3,440,256]{3,2,1,0:T(8,128)(2,1)}), bf16[8,3,440,256]{3,2,1,0:T(8,128)(2,1)}, u32[]{:S(2)}, u32[]{:S(2)}) %all-to-all-start.1) | async-done | bytes 5406752 | tf_op jit(solution)/shard_map/all_to_all | solution.py:41
  361.9 44.5 %all-gather.8.cloned.1.call-done = bf16[2048,2048]{1,0:T(8,128)(2,1)} async-done(((bf16[64,2048]{1,0:T(8,128)(2,1)}), bf16[2048,2048]{1,0:T(8,128)(2,1)}) %all-gather.8.cloned.1.call-update) | async-done | bytes 8388624 | tf_op jit(solution)/shard_map/all_gather | solution.py:33
  406.4 5.8 fusion.73
  412.6 5.7 fusion.72
  418.3 5.8 fusion.71
  424.3 11.5 %multiply_convert_fusion = (bf16[2048,440]{0,1:T(8,128)(2,1)}, bf16[2048,440]{0,1:T(8,128)(2,1)S(1)}, bf16[2048,440]{0,1:T(8,128)(2,1)}, f32[2048,440]{0,1:T(8,128)}, f32[2048,440]{0,1:T(8,128)}) fusion(f32[2048,176]{0,1:T(8,128)S(1)} %broadcast_in_dim.169, f32[2048,264]{0,1:T(8,128)S(1)} %copy-done.11, f32[2048,440]{0,1:T(8,128)} %fusion.71, ...), kind=kOutput, calls=%fused_computation.24 | convolution fusion | flops 3709009920 | bytes 33619968 | tf_op jit(solution)/shard_map/dot_general | solution.py:21
  438.5 8.2 fusion.74
  446.6 11.2 %add_convert_fusion = bf16[2048,2048]{1,0:T(8,128)(2,1)} fusion(f32[2048,2048]{1,0:T(8,128)} %fusion.74, f32[2048]{0:T(1024)S(1)} %convert_element_type.270, f32[2048]{0:T(1024)S(1)} %subtract_multiply_fusion, bf16[2048,440]{0,1:T(8,128)(2,1)} %get-tuple-element.98, bf16[440,2048]{1,0:T(8,128)(2,1)S(1)} %bitcast.231), kind=kOutput, calls=%fused_computation.2 | convolution fusion | flops 3707764736 | bytes 28786688 | tf_op jit(solution)/shard_map/dot_general | solution.py:29
  458.4 9.9 convolution_convert_fusion.1
  468.3 138.6 %reduce-scatter.13.cloned.1.call-done = bf16[64,2048]{1,0:T(8,128)(2,1)} async-done(((bf16[2048,2048]{1,0:T(8,128)(2,1)}), bf16[64,2048]{1,0:T(8,128)(2,1)}) %reduce-scatter.13.cloned.1.call-update) | async-done | bytes 262160 | tf_op jit(solution)/shard_map/reduce_scatter | solution.py:37
  610.1 143.7 %reduce-scatter.9.cloned.1.call-done = bf16[256,2048]{1,0:T(8,128)(2,1)} async-done(((bf16[2048,2048]{1,0:T(8,128)(2,1)}), bf16[256,2048]{1,0:T(8,128)(2,1)}) %reduce-scatter.9.cloned.1.call-update) | async-done | bytes 1048592 | tf_op jit(solution)/shard_map/reduce_scatter | solution.py:184
  753.8 3.4 fusion.25
  767.8 6.2 fusion.5
  777.6 4.5 convolution_convert_fusion
  782.2 8.4 pad_maximum_fusion
  790.6 7.8 fusion.13
  800.8 7.5 convolution_convert_fusion.4
  810.3 4.1 convolution_convert_fusion.3
  818.3 4.9 all-to-all-start.3
  824.1 5.1 multiply_reduce_fusion
  829.2 179.2 %all-to-all-done.3 = bf16[8,3,440,256]{3,2,1,0:T(8,128)(2,1)} async-done(((bf16[8,3,440,256]{3,2,1,0:T(8,128)(2,1)}), bf16[8,3,440,256]{3,2,1,0:T(8,128)(2,1)}, u32[]{:S(2)}, u32[]{:S(2)}) %all-to-all-start.3) | async-done | bytes 5406752 | tf_op jit(solution)/shard_map/all_to_all | solution.py:41
  1008.4 3.5 all-to-all-start
  1011.9 3.5 copy_convert_fusion
  1015.4 4.2 slice_bitcast_fusion
  1044.7 3.5 all-to-all-start.2
  1048.2 41.3 %psum.7 = f32[8,1280]{1,0:T(8,128)S(1)} all-reduce(f32[8,1280]{1,0:T(8,128)S(1)} %pad_maximum_fusion.4), channel_id=1, replica_groups=mesh['dp'=8,'tensor'=4] {'dp','tensor'}, use_global_device_ids=true, to_apply=%region_19.20 | all-reduce | flops 10240 | bytes 81920 | tf_op jit(solution)/shard_map/psum | solution.py:264
  (244 shorter events, 105.4 us)
Async XLA Ops:
  8.0 132.9 %all-gather.6.cloned.1.call-start = ((), (), s32[]{:S(2)}) async-start(), calls=%async_computation.10 | async-start | bytes 9437184 | tf_op jit(solution)/shard_map/all_gather | solution.py:114
  11.7 35.6 %copy-start.4 = (bf16[2,128,2048]{2,1,0:T(8,128)(2,1)S(1)}, bf16[2,128,2048]{2,1,0:T(8,128)(2,1)}, u32[]{:S(2)}) copy-start(bf16[2,128,2048]{2,1,0:T(8,128)(2,1)} %param.21) | copy-start | bytes 3145732
  12.8 169.9 %reduce-scatter.7.cloned.1.call-start = ((), (), s32[]{:S(2)}) async-start(), calls=%async_computation.11 | async-start | bytes 2621440 | tf_op jit(solution)/shard_map/reduce_scatter | solution.py:162
  148.0 5.2 copy-start.12
  149.5 3.8 copy-start.36
  149.5 4.3 copy-start.25
  149.5 4.3 copy-start.26
  153.2 205.8 %all-gather.10.cloned.1.call-start = ((), (), s32[]{:S(2)}) async-start(), calls=%async_computation.13 | async-start | bytes 9191424 | tf_op jit(solution)/shard_map/all_gather | solution.py:33
  153.8 28.9 %copy-start.27 = (pred[256]{0:T(512)(128)(4,1)}, pred[256]{0:T(512)(128)(4,1)S(1)}, u32[]{:S(2)}) copy-start(pred[256]{0:T(512)(128)(4,1)S(1)} %get-tuple-element.131) | copy-start | bytes 772
  156.4 250.0 %all-gather.8.cloned.1.call-start = ((), (), s32[]{:S(2)}) async-start(), calls=%async_computation.12 | async-start | bytes 8650752 | tf_op jit(solution)/shard_map/all_gather | solution.py:33
  200.5 151.3 %all-to-all-start.1 = ((bf16[8,3,440,256]{3,2,1,0:T(8,128)(2,1)}), bf16[8,3,440,256]{3,2,1,0:T(8,128)(2,1)}, u32[]{:S(2)}, u32[]{:S(2)}) async-start(bf16[8,3,440,256]{3,2,1,0:T(8,128)(2,1)} %pad_maximum_fusion.1), calls=%async_computation.2 | async-start | bytes 10813440 | tf_op jit(solution)/shard_map/all_to_all | solution.py:41
  206.0 400.9 %reduce-scatter.13.cloned.1.call-start = ((), (), s32[]{:S(2)}) async-start(), calls=%async_computation.16 | async-start | bytes 8650752 | tf_op jit(solution)/shard_map/reduce_scatter | solution.py:37
  406.4 5.8 copy-start
  406.4 6.3 copy-start.15
  412.6 5.7 copy-start.16
  418.3 6.0 copy-start.11
  418.3 6.0 copy-start.14
  435.8 10.8 copy-start.37
  457.9 295.8 %reduce-scatter.9.cloned.1.call-start = ((), (), s32[]{:S(2)}) async-start(), calls=%async_computation.14 | async-start | bytes 9437184 | tf_op jit(solution)/shard_map/reduce_scatter | solution.py:184
  468.3 285.6 %all-gather.12.cloned.1.call-start = ((), (), s32[]{:S(2)}) async-start(), calls=%async_computation.17 | async-start | bytes 1310720 | tf_op jit(solution)/shard_map/all_gather | solution.py:217
  610.0 428.9 %reduce-scatter.11.cloned.1.call-start = ((), (), s32[]{:S(2)}) async-start(), calls=%async_computation.15 | async-start | bytes 1310720 | tf_op jit(solution)/shard_map/reduce_scatter | solution.py:185
  753.8 287.0 %reduce-scatter.15.cloned.1.call-start = ((), (), s32[]{:S(2)}) async-start(), calls=%async_computation.18 | async-start | bytes 2621440 | tf_op jit(solution)/shard_map/reduce_scatter | solution.py:247
  774.0 317.8 %reduce-scatter.17.cloned.1.call-start = ((), (), s32[]{:S(2)}) async-start(), calls=%async_computation.19 | async-start | bytes 9437184 | tf_op jit(solution)/shard_map/reduce_scatter | solution.py:243
  798.4 10.8 slice-start
  800.8 8.4 slice-start.1
  818.3 5.8 copy-start.31
  818.3 190.1 %all-to-all-start.3 = ((bf16[8,3,440,256]{3,2,1,0:T(8,128)(2,1)}), bf16[8,3,440,256]{3,2,1,0:T(8,128)(2,1)}, u32[]{:S(2)}, u32[]{:S(2)}) async-start(bf16[8,3,440,256]{3,2,1,0:T(8,128)(2,1)} %maximum_bitcast_fusion), calls=%async_computation.9 | async-start | bytes 10813440 | tf_op jit(solution)/shard_map/all_to_all | solution.py:41
  1008.4 30.5 %all-to-all-start = ((f32[64,4,512]{2,0,1:T(8,128)}), f32[64,4,512]{2,0,1:T(8,128)S(1)}, u32[]{:S(2)}, u32[]{:S(2)}) async-start(f32[64,4,512]{2,0,1:T(8,128)} %bitcast.197), calls=%async_computation.1 | async-start | bytes 1048576 | tf_op jit(solution)/shard_map/all_to_all | solution.py:271
  1035.6 5.2 copy-start.24
  1035.6 6.7 copy-start.7
  1042.3 48.6 %copy-start.32 = (pred[2,128]{1,0:T(4,128)(4,1)S(1)}, pred[2,128]{1,0:T(4,128)(4,1)}, u32[]{:S(2)}) copy-start(pred[2,128]{1,0:T(4,128)(4,1)} %get-tuple-element.130) | copy-start | bytes 772
  1044.7 46.2 %all-to-all-start.2 = ((f32[64,4,512]{2,0,1:T(8,128)}), f32[64,4,512]{2,0,1:T(8,128)S(1)}, u32[]{:S(2)}, u32[]{:S(2)}) async-start(f32[64,4,512]{2,0,1:T(8,128)} %bitcast.196), calls=%async_computation.7 | async-start | bytes 1048576 | tf_op jit(solution)/shard_map/all_to_all | solution.py:271
  (24 other events, 49.3 us)
Sparse Core Ops, SparseCore 0:
  13.0 127.8 all-gather.5
  153.3 29.3 reduce-scatter.6
  610.1 12.5 all-gather.11
  753.9 23.8 reduce-scatter.10
  780.2 31.1 reduce-scatter.14
  814.9 251.4 reduce-scatter.16
Sparse Core Ops, SparseCore 1:
  157.1 113.9 all-gather.9
  274.4 131.9 all-gather.7
  458.0 148.8 reduce-scatter.12
  610.5 143.2 reduce-scatter.8
where the time goes:
time: 1110 us; the launch traced here: 1100 us
  waiting for transfers between devices  770 us (69%)
  matrix products  111 us (10%)
  blocking collectives  74.8 us (7%)
  local copies, waits for them, and re-layouts  66.3 us (6%)
  other arithmetic  47.6 us (4%)
  starting transfers between devices  18.5 us (2%)
  between operations  16.9 us (2%)
    all_to_all x2, waiting for transfers between devices, exchange_dp(): return lax.all_to_all(value, 'dp', 0, 0, tiled=False)  325 us
    reduce_scatter x1, waiting for transfers between devices, per_device(): mixed = lax.psum_scatter(mixed, 'dp', scatter_dimension=0, tiled=True)  144 us
    reduce_scatter x1, waiting for transfers between devices, scatter_all(): return lax.psum_scatter(value, ALL, scatter_dimension=0, tiled=True)  139 us
    all_gather x1, waiting for transfers between devices, per_device(): attn_weights = lax.all_gather(attn_weights, 'dp', axis=0, tiled=True)  91.7 us
    all_gather x2, waiting for transfers between devices, gather_all(): return lax.all_gather(value, ALL, axis=0, tiled=True)  44.5 us
    psum x1, blocking collectives, per_device(): pack = lax.psum(pack, ALL)  41.3 us
    dot_general x6, matrix products, nn(): lax.dot_general(left, right, (((1,), (0,)), ((), ())), preferred_element_...  40.1 us
    dot_general x6, matrix products, nt(): lax.dot_general(left, right, (((1,), (1,)), ((), ())), preferred_element_...  38.7 us
  transfers between devices with their start and end apart: 14, of which 7 were waited for; matrix products, arithmetic and copies ran while one was open for 13% of the time, Pallas kernels for 0%

commit v1 on v0

--- a/solution.py
+++ b/solution.py
@@ -11,6 +11,27 @@
 BF16 = jnp.bfloat16
 F32 = jnp.float32
 ALL = ("dp", "tensor")
+
+
+def collect(x, axis, dim):
+    peers, position, rows = (lax.axis_size(axis), lax.axis_index(axis), x.shape[dim])
+    ahead = [(i, (i + 1) % peers) for i in range(peers)]
+    behind = [(i, (i - 1) % peers) for i in range(peers)]
+    out = jnp.zeros((*x.shape[:dim], peers * rows, *x.shape[dim + 1 :]), x.dtype)
+    out = lax.dynamic_update_slice_in_dim(out, x, position * rows, axis=dim)
+    from_left = from_right = x
+    half = peers // 2
+    for step in range(1, half + 1):
+        from_left = lax.ppermute(from_left, axis, ahead)
+        out = lax.dynamic_update_slice_in_dim(
+            out, from_left, (position - step) % peers * rows, axis=dim
+        )
+        if step < peers - half:
+            from_right = lax.ppermute(from_right, axis, behind)
+            out = lax.dynamic_update_slice_in_dim(
+                out, from_right, (position + step) % peers * rows, axis=dim
+            )
+    return out
 
 
 def normalize(values, gain):
@@ -111,7 +132,7 @@
         ],
         axis=1,
     )
-    attn_weights = lax.all_gather(attn_weights, "dp", axis=0, tiled=True)
+    attn_weights = collect(attn_weights, "dp", 0)
     weight_qkv = attn_weights[:, : 3 * head_cols]
     weight_o = attn_weights[:, 3 * head_cols :]
 

time: 1110 us -> 1180 us (1.063)
  waiting for transfers between devices: 770 us -> 793 us
  blocking collectives: 74.8 us -> 90.4 us
  starting transfers between devices: 18.5 us -> 31.4 us
    ppermute x0 -> x7, waiting for transfers between devices: none -> 115 us  [the longest x4 76.3 us: collect(): from_left = lax.ppermute(from_left, axis, ahead)]
    all_gather x1 -> x0, waiting for transfers between devices: 91.7 us -> none  [per_device(): attn_weights = lax.all_gather(attn_weights, 'dp', axis=0, tiled=True)]
    all_gather x1, blocking collectives: 33.5 us -> 48.8 us  [per_device(): small = lax.all_gather(small[None, :], 'dp', axis=0, tiled=True)]
    ppermute x0 -> x7, starting transfers between devices: none -> 13.1 us  [the longest x4 8 us: collect(): from_left = lax.ppermute(from_left, axis, ahead)]
  transfers between devices with their start and end apart: 14 -> 20, of which waited for: 7 -> 10; matrix products, arithmetic and copies ran while one was open for 13% -> 13% of each run, Pallas kernels for 0% -> 0%
where the time goes in v1:
time: 1180 us; the launch traced here: 1170 us
  waiting for transfers between devices  793 us (67%)
  matrix products  111 us (9%)
  blocking collectives  90.4 us (8%)
  local copies, waits for them, and re-layouts  76.5 us (6%)
  other arithmetic  50.4 us (4%)
  starting transfers between devices  31.4 us (3%)
  between operations  16.8 us (1%)
    all_to_all x2, waiting for transfers between devices, exchange_dp(): return lax.all_to_all(value, 'dp', 0, 0, tiled=False)  326 us
    reduce_scatter x1, waiting for transfers between devices, per_device(): mixed = lax.psum_scatter(mixed, 'dp', scatter_dimension=0, tiled=True)  144 us
    reduce_scatter x1, waiting for transfers between devices, scatter_all(): return lax.psum_scatter(value, ALL, scatter_dimension=0, tiled=True)  139 us
    ppermute x4, waiting for transfers between devices, collect(): from_left = lax.ppermute(from_left, axis, ahead)  76.3 us
    all_gather x1, blocking collectives, per_device(): small = lax.all_gather(small[None, :], 'dp', axis=0, tiled=True)  48.8 us
    all_gather x2, waiting for transfers between devices, gather_all(): return lax.all_gather(value, ALL, axis=0, tiled=True)  44.5 us
    psum x1, blocking collectives, per_device(): pack = lax.psum(pack, ALL)  41.6 us
    dot_general x6, matrix products, nn(): lax.dot_general(left, right, (((1,), (0,)), ((), ())), preferred_element_...  40.2 us
  transfers between devices with their start and end apart: 20, of which 10 were waited for; matrix products, arithmetic and copies ran while one was open for 13% of the time, Pallas kernels for 0%

profile of v1, /device:TPU:0, one launch (start us, length us, event | category | flops | bytes accessed | tf_op | source)
XLA Modules:
  0.0 1170.1 jit_solution(388563664363587503)
XLA Ops:
  12.7 4.4 broadcast_in_dim.155
  24.6 42.2 %collective-permute-done = bf16[256,2048]{0,1:T(8,128)(2,1)S(1)} collective-permute-done((bf16[256,2048]{0,1:T(8,128)(2,1)}, bf16[256,2048]{0,1:T(8,128)(2,1)S(1)}, u32[]{:S(2)}, u32[]{:S(2)}) %collective-permute-start) | collective-permute-done | bytes 1048608 | tf_op jit(solution)/shard_map/ppermute | solution.py:25
  69.6 48.8 %all-gather = bf16[8,1,896]{2,1,0:T(2,128)(2,1)S(1)} all-gather(bf16[1,1,896]{2,1,0:T(2,128)(2,1)S(1)} %bitcast.258), channel_id=1, replica_groups=mesh['dp'=8,'tensor'=4] {'dp'}, dimensions={0}, use_global_device_ids=true | all-gather | bytes 16128 | tf_op jit(solution)/shard_map/all_gather | solution.py:114
  122.9 38.2 %collective-permute-done.3 = bf16[256,2048]{0,1:T(8,128)(2,1)} collective-permute-done((bf16[256,2048]{0,1:T(8,128)(2,1)S(1)}, bf16[256,2048]{0,1:T(8,128)(2,1)}, u32[]{:S(2)}, u32[]{:S(2)}) %collective-permute-start.3) | collective-permute-done | bytes 1048608 | tf_op jit(solution)/shard_map/ppermute | solution.py:30
  162.4 16.6 %collective-permute-done.4 = bf16[256,2048]{0,1:T(8,128)(2,1)S(1)} collective-permute-done((bf16[256,2048]{0,1:T(8,128)(2,1)}, bf16[256,2048]{0,1:T(8,128)(2,1)S(1)}, u32[]{:S(2)}, u32[]{:S(2)}) %collective-permute-start.4) | collective-permute-done | bytes 1048608 | tf_op jit(solution)/shard_map/ppermute | solution.py:25
  189.3 17.5 %collective-permute-done.6 = bf16[256,2048]{0,1:T(8,128)(2,1)S(1)} collective-permute-done((bf16[256,2048]{0,1:T(8,128)(2,1)S(1)}, bf16[256,2048]{0,1:T(8,128)(2,1)S(1)}, u32[]{:S(2)}, u32[]{:S(2)}) %collective-permute-start.6) | collective-permute-done | bytes 1048608 | tf_op jit(solution)/shard_map/ppermute | solution.py:25
  207.9 4.6 fusion.7
  216.6 3.6 fusion.18
  223.5 25.4 %reduce-scatter.7.cloned.1.call-done = f32[64,2048]{1,0:T(8,128)} async-done(((f32[256,2048]{1,0:T(8,128)}), f32[64,2048]{1,0:T(8,128)}) %reduce-scatter.7.cloned.1.call-update) | async-done | bytes 524304 | tf_op jit(solution)/shard_map/reduce_scatter | solution.py:183
  265.0 5.5 all-to-all-start.1
  270.8 147.0 %all-to-all-done.1 = bf16[8,3,440,256]{3,2,1,0:T(8,128)(2,1)} async-done(((bf16[8,3,440,256]{3,2,1,0:T(8,128)(2,1)}), bf16[8,3,440,256]{3,2,1,0:T(8,128)(2,1)}, u32[]{:S(2)}, u32[]{:S(2)}) %all-to-all-start.1) | async-done | bytes 5406752 | tf_op jit(solution)/shard_map/all_to_all | solution.py:62
  428.0 44.5 %all-gather.5.cloned.1.call-done = bf16[2048,2048]{1,0:T(8,128)(2,1)} async-done(((bf16[64,2048]{1,0:T(8,128)(2,1)}), bf16[2048,2048]{1,0:T(8,128)(2,1)}) %all-gather.5.cloned.1.call-update) | async-done | bytes 8388624 | tf_op jit(solution)/shard_map/all_gather | solution.py:54
  472.5 5.8 fusion.75
  478.7 5.8 fusion.74
  484.6 5.8 fusion.73
  490.5 11.7 %multiply_convert_fusion = (bf16[2048,440]{0,1:T(8,128)(2,1)}, bf16[2048,440]{0,1:T(8,128)(2,1)S(1)}, bf16[2048,440]{0,1:T(8,128)(2,1)}, f32[2048,440]{0,1:T(8,128)}, f32[2048,440]{0,1:T(8,128)}) fusion(f32[2048,176]{0,1:T(8,128)S(1)} %broadcast_in_dim.173, f32[2048,264]{0,1:T(8,128)S(1)} %copy-done.11, f32[2048,440]{0,1:T(8,128)} %fusion.73, ...), kind=kOutput, calls=%fused_computation.24 | convolution fusion | flops 3709009920 | bytes 33619968 | tf_op jit(solution)/shard_map/dot_general | solution.py:42
  504.8 8.2 fusion.76
  513.0 11.2 add_convert_fusion
  524.5 9.9 convolution_convert_fusion.1
  534.5 138.8 %reduce-scatter.13.cloned.1.call-done = bf16[64,2048]{1,0:T(8,128)(2,1)} async-done(((bf16[2048,2048]{1,0:T(8,128)(2,1)}), bf16[64,2048]{1,0:T(8,128)(2,1)}) %reduce-scatter.13.cloned.1.call-update) | async-done | bytes 262160 | tf_op jit(solution)/shard_map/reduce_scatter | solution.py:58
  676.5 143.7 %reduce-scatter.9.cloned.1.call-done = bf16[256,2048]{1,0:T(8,128)(2,1)} async-done(((bf16[2048,2048]{1,0:T(8,128)(2,1)}), bf16[256,2048]{1,0:T(8,128)(2,1)}) %reduce-scatter.9.cloned.1.call-update) | async-done | bytes 1048592 | tf_op jit(solution)/shard_map/reduce_scatter | solution.py:205
  835.2 6.0 fusion.5
  844.8 4.5 convolution_convert_fusion
  849.4 8.7 pad_maximum_fusion
  858.1 7.8 fusion.13
  867.4 7.6 convolution_convert_fusion.4
  876.5 4.1 convolution_convert_fusion.3
  884.6 4.9 all-to-all-start.3
  890.4 5.1 multiply_reduce_fusion
  895.4 179.3 %all-to-all-done.3 = bf16[8,3,440,256]{3,2,1,0:T(8,128)(2,1)} async-done(((bf16[8,3,440,256]{3,2,1,0:T(8,128)(2,1)}), bf16[8,3,440,256]{3,2,1,0:T(8,128)(2,1)}, u32[]{:S(2)}, u32[]{:S(2)}) %all-to-all-start.3) | async-done | bytes 5406752 | tf_op jit(solution)/shard_map/all_to_all | solution.py:62
  1081.7 4.2 slice_bitcast_fusion
  1113.1 41.6 %psum.7 = f32[8,1280]{1,0:T(8,128)S(1)} all-reduce(f32[8,1280]{1,0:T(8,128)S(1)} %pad_maximum_fusion.4), channel_id=1, replica_groups=mesh['dp'=8,'tensor'=4] {'dp','tensor'}, use_global_device_ids=true, to_apply=%region_19.20 | all-reduce | flops 10240 | bytes 81920 | tf_op jit(solution)/shard_map/psum | solution.py:285
  (263 shorter events, 140.3 us)
Async XLA Ops:
  8.0 240.8 %reduce-scatter.7.cloned.1.call-start = ((), (), s32[]{:S(2)}) async-start(), calls=%async_computation.10 | async-start | bytes 2621440 | tf_op jit(solution)/shard_map/reduce_scatter | solution.py:183
  12.7 56.5 %copy-start.33 = (f32[256]{0:T(256)S(1)}, f32[256]{0:T(256)}, u32[]{:S(2)}) copy-start(f32[256]{0:T(256)} %param.26) | copy-start | bytes 3076
  12.7 56.5 %copy-start.34 = (f32[256]{0:T(256)S(1)}, f32[256]{0:T(256)}, u32[]{:S(2)}) copy-start(f32[256]{0:T(256)} %param.33) | copy-start | bytes 3076
  12.7 56.6 %copy-start.35 = (f32[256]{0:T(256)S(1)}, f32[256]{0:T(256)}, u32[]{:S(2)}) copy-start(f32[256]{0:T(256)} %param.40) | copy-start | bytes 3076
  12.7 56.6 %copy-start.29 = (f32[4,16]{1,0:T(4,128)S(1)}, f32[4,16]{1,0:T(4,128)}, u32[]{:S(2)}) copy-start(f32[4,16]{1,0:T(4,128)} %param.28) | copy-start | bytes 772
  12.7 56.7 %copy-start.30 = (f32[4,16]{1,0:T(4,128)S(1)}, f32[4,16]{1,0:T(4,128)}, u32[]{:S(2)}) copy-start(f32[4,16]{1,0:T(4,128)} %param.31) | copy-start | bytes 772
  17.1 103.6 %copy-start.4 = (bf16[2,128,2048]{2,1,0:T(8,128)(2,1)S(1)}, bf16[2,128,2048]{2,1,0:T(8,128)(2,1)}, u32[]{:S(2)}) copy-start(bf16[2,128,2048]{2,1,0:T(8,128)(2,1)} %param.21) | copy-start | bytes 3145732
  18.6 48.2 %collective-permute-start = (bf16[256,2048]{0,1:T(8,128)(2,1)}, bf16[256,2048]{0,1:T(8,128)(2,1)S(1)}, u32[]{:S(2)}, u32[]{:S(2)}) collective-permute-start(bf16[256,2048]{0,1:T(8,128)(2,1)} %get-tuple-element.111), channel_id=1, source_target_pairs={{0,4},{4,8},{8,12},{12,16},{16,20},{20,24},{24,28},{28,0},{1,5},{5... | collective-permute-start | bytes 3145736 | tf_op jit(solution)/shard_map/ppermute | solution.py:25
  21.6 96.8 %collective-permute-start.1 = (bf16[256,2048]{0,1:T(8,128)(2,1)}, bf16[256,2048]{0,1:T(8,128)(2,1)S(1)}, u32[]{:S(2)}, u32[]{:S(2)}) collective-permute-start(bf16[256,2048]{0,1:T(8,128)(2,1)} %get-tuple-element.111), channel_id=1, source_target_pairs={{0,28},{4,0},{8,4},{12,8},{16,12},{20,16},{24,20},{28,24},{1,29},{... | collective-permute-start | bytes 3145736 | tf_op jit(solution)/shard_map/ppermute | solution.py:30
  66.8 54.5 %copy-start.18 = (bf16[256,2048]{0,1:T(8,128)(2,1)}, bf16[256,2048]{0,1:T(8,128)(2,1)S(1)}, u32[]{:S(2)}) copy-start(bf16[256,2048]{0,1:T(8,128)(2,1)S(1)} %collective-permute-done) | copy-start | bytes 3145732
  66.8 54.2 %collective-permute-start.2 = (bf16[256,2048]{0,1:T(8,128)(2,1)S(1)}, bf16[256,2048]{0,1:T(8,128)(2,1)}, u32[]{:S(2)}, u32[]{:S(2)}) collective-permute-start(bf16[256,2048]{0,1:T(8,128)(2,1)S(1)} %collective-permute-done), channel_id=1, source_target_pairs={{0,4},{4,8},{8,12},{12,16},{16,20},{20,24},{24,28},{28,0},{1,5},{5... | collective-permute-start | bytes 3145736 | tf_op jit(solution)/shard_map/ppermute | solution.py:25
  118.4 42.7 %collective-permute-start.3 = (bf16[256,2048]{0,1:T(8,128)(2,1)S(1)}, bf16[256,2048]{0,1:T(8,128)(2,1)}, u32[]{:S(2)}, u32[]{:S(2)}) collective-permute-start(bf16[256,2048]{0,1:T(8,128)(2,1)S(1)} %collective-permute-done.1), channel_id=1, source_target_pairs={{0,28},{4,0},{8,4},{12,8},{16,12},{20,16},{24,20},{28,24},{1,29},{... | collective-permute-start | bytes 3145736 | tf_op jit(solution)/shard_map/ppermute | solution.py:30
  120.4 42.0 %copy-start.23 = (f32[1,2,8,128]{3,1,2,0:T(2,128)}, f32[1,2,8,128]{3,1,2,0:T(2,128)S(1)}, u32[]{:S(2)}) copy-start(f32[1,2,8,128]{3,1,2,0:T(2,128)S(1)} %copy.189) | copy-start | bytes 24580
  121.0 57.9 %collective-permute-start.4 = (bf16[256,2048]{0,1:T(8,128)(2,1)}, bf16[256,2048]{0,1:T(8,128)(2,1)S(1)}, u32[]{:S(2)}, u32[]{:S(2)}) collective-permute-start(bf16[256,2048]{0,1:T(8,128)(2,1)} %collective-permute-done.2), channel_id=1, source_target_pairs={{0,4},{4,8},{8,12},{12,16},{16,20},{20,24},{24,28},{28,0},{1,5},{5... | collective-permute-start | bytes 3145736 | tf_op jit(solution)/shard_map/ppermute | solution.py:25
  121.3 40.0 %copy-start.19 = (bf16[256,2048]{0,1:T(8,128)(2,1)S(1)}, bf16[256,2048]{0,1:T(8,128)(2,1)}, u32[]{:S(2)}) copy-start(bf16[256,2048]{0,1:T(8,128)(2,1)} %copy-done.18) | copy-start | bytes 3145732
  161.1 27.1 %collective-permute-start.5 = (bf16[256,2048]{0,1:T(8,128)(2,1)}, bf16[256,2048]{0,1:T(8,128)(2,1)S(1)}, u32[]{:S(2)}, u32[]{:S(2)}) collective-permute-start(bf16[256,2048]{0,1:T(8,128)(2,1)} %collective-permute-done.3), channel_id=1, source_target_pairs={{0,28},{4,0},{8,4},{12,8},{16,12},{20,16},{24,20},{28,24},{1,29},{... | collective-permute-start | bytes 3145736 | tf_op jit(solution)/shard_map/ppermute | solution.py:30
  179.0 27.8 %collective-permute-start.6 = (bf16[256,2048]{0,1:T(8,128)(2,1)S(1)}, bf16[256,2048]{0,1:T(8,128)(2,1)S(1)}, u32[]{:S(2)}, u32[]{:S(2)}) collective-permute-start(bf16[256,2048]{0,1:T(8,128)(2,1)S(1)} %collective-permute-done.4), channel_id=1, source_target_pairs={{0,4},{4,8},{8,12},{12,16},{16,20},{20,24},{24,28},{28,0},{1,5},{5... | collective-permute-start | bytes 3145736 | tf_op jit(solution)/shard_map/ppermute | solution.py:25
  220.2 204.9 %all-gather.7.cloned.1.call-start = ((), (), s32[]{:S(2)}) async-start(), calls=%async_computation.12 | async-start | bytes 9191424 | tf_op jit(solution)/shard_map/all_gather | solution.py:54
  220.9 33.2 %copy-start.27 = (pred[256]{0:T(512)(128)(4,1)}, pred[256]{0:T(512)(128)(4,1)S(1)}, u32[]{:S(2)}) copy-start(pred[256]{0:T(512)(128)(4,1)S(1)} %get-tuple-element.133) | copy-start | bytes 772
  223.4 249.1 %all-gather.5.cloned.1.call-start = ((), (), s32[]{:S(2)}) async-start(), calls=%async_computation.11 | async-start | bytes 8650752 | tf_op jit(solution)/shard_map/all_gather | solution.py:54
  265.0 152.9 %all-to-all-start.1 = ((bf16[8,3,440,256]{3,2,1,0:T(8,128)(2,1)}), bf16[8,3,440,256]{3,2,1,0:T(8,128)(2,1)}, u32[]{:S(2)}, u32[]{:S(2)}) async-start(bf16[8,3,440,256]{3,2,1,0:T(8,128)(2,1)} %pad_maximum_fusion.1), calls=%async_computation.2 | async-start | bytes 10813440 | tf_op jit(solution)/shard_map/all_to_all | solution.py:62
  270.5 402.8 %reduce-scatter.13.cloned.1.call-start = ((), (), s32[]{:S(2)}) async-start(), calls=%async_computation.15 | async-start | bytes 8650752 | tf_op jit(solution)/shard_map/reduce_scatter | solution.py:58
  502.2 10.8 copy-start.37
  524.3 295.8 %reduce-scatter.9.cloned.1.call-start = ((), (), s32[]{:S(2)}) async-start(), calls=%async_computation.13 | async-start | bytes 9437184 | tf_op jit(solution)/shard_map/reduce_scatter | solution.py:205
  534.4 285.8 %all-gather.9.cloned.1.call-start = ((), (), s32[]{:S(2)}) async-start(), calls=%async_computation.16 | async-start | bytes 1310720 | tf_op jit(solution)/shard_map/all_gather | solution.py:238
  676.4 427.4 %reduce-scatter.11.cloned.1.call-start = ((), (), s32[]{:S(2)}) async-start(), calls=%async_computation.14 | async-start | bytes 1310720 | tf_op jit(solution)/shard_map/reduce_scatter | solution.py:206
  820.1 285.6 %reduce-scatter.15.cloned.1.call-start = ((), (), s32[]{:S(2)}) async-start(), calls=%async_computation.17 | async-start | bytes 2621440 | tf_op jit(solution)/shard_map/reduce_scatter | solution.py:268
  841.2 315.8 %reduce-scatter.17.cloned.1.call-start = ((), (), s32[]{:S(2)}) async-start(), calls=%async_computation.18 | async-start | bytes 9437184 | tf_op jit(solution)/shard_map/reduce_scatter | solution.py:264
  884.6 190.2 %all-to-all-start.3 = ((bf16[8,3,440,256]{3,2,1,0:T(8,128)(2,1)}), bf16[8,3,440,256]{3,2,1,0:T(8,128)(2,1)}, u32[]{:S(2)}, u32[]{:S(2)}) async-start(bf16[8,3,440,256]{3,2,1,0:T(8,128)(2,1)} %maximum_bitcast_fusion), calls=%async_computation.9 | async-start | bytes 10813440 | tf_op jit(solution)/shard_map/all_to_all | solution.py:62
  1074.7 29.0 %all-to-all-start = ((f32[64,4,512]{2,0,1:T(8,128)}), f32[64,4,512]{2,0,1:T(8,128)S(1)}, u32[]{:S(2)}, u32[]{:S(2)}) async-start(f32[64,4,512]{2,0,1:T(8,128)} %bitcast.197), calls=%async_computation.1 | async-start | bytes 1048576 | tf_op jit(solution)/shard_map/all_to_all | solution.py:292
  1103.8 52.4 %copy-start.32 = (pred[2,128]{1,0:T(4,128)(4,1)S(1)}, pred[2,128]{1,0:T(4,128)(4,1)}, u32[]{:S(2)}) copy-start(pred[2,128]{1,0:T(4,128)(4,1)} %get-tuple-element.132) | copy-start | bytes 772
  1109.6 46.5 %all-to-all-start.2 = ((f32[64,4,512]{2,0,1:T(8,128)}), f32[64,4,512]{2,0,1:T(8,128)S(1)}, u32[]{:S(2)}, u32[]{:S(2)}) async-start(f32[64,4,512]{2,0,1:T(8,128)} %bitcast.196), calls=%async_computation.7 | async-start | bytes 1048576 | tf_op jit(solution)/shard_map/all_to_all | solution.py:292
  (30 other events, 137.7 us)
Sparse Core Ops, SparseCore 0:
  220.3 28.4 reduce-scatter.6
  676.5 12.5 all-gather.8
  820.3 23.9 reduce-scatter.10
  846.6 31.1 reduce-scatter.14
  881.3 253.3 reduce-scatter.16
Sparse Core Ops, SparseCore 1:
  224.2 113.1 all-gather.6
  340.7 131.7 all-gather.4
  524.4 148.8 reduce-scatter.12
  676.9 143.1 reduce-scatter.8
